TPU v7x, 64 devices: a 2x2x8 block of a 4x4x8 slice. The times are simulated.
64 devices in a mesh: dp: 4 (over x, y), sp: 16 (over z, core).
Axes of the slice: x: 2, y: 2, z: 8, core: 2. Of those that a mesh axis runs over, the one named last changes fastest.
The devices are a block of a 4x4x8 slice.
Arguments:
- pixels: bfloat16 [128, 384, 512, 3], P('dp', 'sp'), parts along dimension 0
- w_stem: bfloat16 [7, 7, 3, 64], replicated
- bn_stem: float32 [2, 64], replicated
- w_a: bfloat16 [6, 3, 3, 64, 64], replicated
- bn_a: float32 [6, 2, 64], replicated
- w_down: bfloat16 [3, 3, 64, 128], replicated
- bn_down: float32 [2, 128], replicated
- w_b: bfloat16 [2, 3, 3, 128, 128], replicated
- bn_b: float32 [2, 2, 128], replicated
Outputs:
- output: bfloat16 [128, 48, 64, 128], P('dp', 'sp'), parts along dimension 0
There are 4 independent parts. A program takes and returns all parts, laid end to end along the dimension named above; an argument that names none is the same for every part.
All inputs are finite; a program needn't handle non-finite values.
Results may differ from a plain program's by a relative error of at most 0.019651.
Values are sent between devices in bfloat16 or wider.
A program may use at most 768 MiB of HBM per device.

v0:
```python
import jax
import jax.numpy as jnp
from jax import lax
from jax.sharding import PartitionSpec as P

BN_EPS = 1e-5
CONV_DIMS = ("NHWC", "HWIO", "NHWC")


def halo_rows(tile, above, below, group):
    pieces = []
    if above:
        pieces.append(lax.ppermute(tile[:, -above:], "sp", [(i, i + 1) for i in range(group - 1)]))
    pieces.append(tile)
    if below:
        pieces.append(lax.ppermute(tile[:, :below], "sp", [(i + 1, i) for i in range(group - 1)]))
    return jnp.concatenate(pieces, axis=1)


def norm_relu(conv_out, bn_pair, count):
    local_sums = jnp.stack([jnp.sum(conv_out, axis=(0, 1, 2)), jnp.sum(conv_out * conv_out, axis=(0, 1, 2))])
    totals = lax.psum(local_sums, "sp")
    ch_mean = totals[0] / count
    ch_var = totals[1] / count - ch_mean * ch_mean
    ch_scale = bn_pair[0] * lax.rsqrt(ch_var + BN_EPS)
    return jnp.maximum((conv_out - ch_mean) * ch_scale + bn_pair[1], 0.0).astype(jnp.bfloat16)


def solution(mesh):
    group = mesh.shape["sp"]

    def conv_layer(hidden, kernel, bn_pair, stride, above, below):
        border = kernel.shape[1] // 2
        conv_out = lax.conv_general_dilated(halo_rows(hidden, above, below, group), kernel, (stride, stride), ((0, 0), (border, border)), dimension_numbers=CONV_DIMS, preferred_element_type=jnp.float32)
        count = conv_out.shape[0] * conv_out.shape[1] * group * conv_out.shape[2]
        return norm_relu(conv_out, bn_pair, count)

    def local_stack(pixels, w_stem, bn_stem, w_a, bn_a, w_down, bn_down, w_b, bn_b):
        hidden = conv_layer(pixels, w_stem, bn_stem, 2, 3, 2)
        hidden = lax.reduce_window(halo_rows(hidden, 1, 0, group), jnp.array(-jnp.inf, hidden.dtype), lax.max, (1, 3, 3, 1), (1, 2, 2, 1), ((0, 0), (0, 0), (1, 1), (0, 0)))
        for layer_idx in range(w_a.shape[0]):
            hidden = conv_layer(hidden, w_a[layer_idx], bn_a[layer_idx], 1, 1, 1)
        hidden = conv_layer(hidden, w_down, bn_down, 2, 1, 0)
        for layer_idx in range(w_b.shape[0]):
            hidden = conv_layer(hidden, w_b[layer_idx], bn_b[layer_idx], 1, 1, 1)
        return hidden

    return jax.shard_map(local_stack, mesh=mesh, in_specs=(P("dp", "sp"),) + (P(),) * 8, out_specs=P("dp", "sp"), check_vma=False)
```

profile of v0, /device:TPU:21, one launch (start us, length us, event | category | flops | bytes accessed | tf_op | source)
XLA Modules:
  0.0 762.0 jit_solution(13180230424696595688)
XLA Ops:
  1.5 5.1 collective-permute-start
  10.7 13.3 %copy.52 = bf16[32,24,512,3]{0,3,2,1:T(4,128)(2,1)} copy(bf16[32,24,512,3]{2,1,3,0:T(8,128)(2,1)} %param.9) | data formatting | bytes 4718592 | tf_op args[0]
  26.3 83.3 %fusion.120 = (f32[64]{0:T(128)S(1)}, f32[64]{0:T(128)S(1)}, f32[32,12,256,64]{3,0,2,1:T(8,128)}) fusion(bf16[7,7,3,64]{3,1,2,0:T(8,128)(2,1)S(1)} %copy-done.15, bf16[32,2,512,3]{0,3,2,1:T(4,128)(2,1)S(1)} %copy.53, bf16[32,24,512,3]{0,3,2,1:T(4,128)(2,1)} %copy.52, bf16[32,3,512,3]{0,3,2,1:T(4,128)(2,1)S(1)} %copy.51), kind=kOutput, calls=%fused_computation.180 | convolution fusion | flops 1870921728 | bytes 28035968 | tf_op jit(solution)/shard_map/conv_general_dilated | solution.py:34
  109.7 26.7 %psum.70 = f32[2,64]{1,0:T(2,128)S(1)} all-reduce(f32[2,64]{1,0:T(2,128)S(1)} %pad_maximum_fusion), channel_id=1, replica_groups=mesh['dp'=4,'sp'=16] {'sp'}, use_global_device_ids=true, to_apply=%region_2.0 | all-reduce | flops 128 | bytes 1024 | tf_op jit(solution)/shard_map/psum | solution.py:22
  136.4 28.0 %maximum_convert_fusion = bf16[32,12,256,64]{3,0,2,1:T(8,128)(2,1)} fusion(f32[32,12,256,64]{3,0,2,1:T(8,128)} %get-tuple-element.49, f32[64]{0:T(128)S(1)} %copy-done.11, f32[64]{0:T(128)S(1)} %fusion.108, f32[64]{0:T(128)S(1)} %multiply_bitcast_fusion.9), kind=kLoop, calls=%fused_computation | loop fusion | flops 31457280 | bytes 37749504 | tf_op jit(solution)/shard_map/convert_element_type | solution.py:26
  170.0 11.7 %collective-permute-done.2 = bf16[32,1,256,64]{2,3,1,0:T(8,128)(2,1)} collective-permute-done((bf16[32,1,256,64]{2,3,1,0:T(8,128)(2,1)S(1)}, bf16[32,1,256,64]{2,3,1,0:T(8,128)(2,1)}, u32[]{:S(2)}, u32[]{:S(2)}) %collective-permute-start.2) | collective-permute-done | bytes 1048608 | tf_op jit(solution)/shard_map/ppermute | solution.py:13
  185.6 12.0 %fusion = bf16[32,6,128,64]{3,0,2,1:T(8,128)(2,1)S(1)} fusion(bf16[32,12,256,64]{3,0,2,1:T(8,128)(2,1)} %maximum_convert_fusion, bf16[32,1,256,64]{3,0,2,1:T(8,128)(2,1)S(1)} %copy.56), kind=kOutput, calls=%fused_computation.2 | output fusion | flops 19398656 | bytes 16777216 | tf_op jit(solution)/shard_map/reduce_window | solution.py:40
  201.7 4.4 collective-permute-start.3
  219.4 13.6 %fusion.126 = (f32[64]{0:T(128)S(1)}, f32[64]{0:T(128)S(1)}, f32[32,6,128,64]{3,0,2,1:T(8,128)}) fusion(bf16[6,3,3,64,64]{4,3,2,1,0:T(8,128)(2,1)} %param.12, bf16[32,1,128,64]{3,0,2,1:T(8,128)(2,1)S(1)} %copy.60, bf16[32,6,128,64]{3,0,2,1:T(8,128)(2,1)} %copy-done.1, bf16[32,1,128,64]{3,0,2,1:T(8,128)(2,1)S(1)} %copy.59), kind=kOutput, calls=%fused_computation.186 | convolution fusion | flops 1819803648 | bytes 13779456 | tf_op jit(solution)/shard_map/conv_general_dilated | solution.py:34
  233.0 22.0 %psum.71 = f32[2,64]{1,0:T(2,128)S(1)} all-reduce(f32[2,64]{1,0:T(2,128)S(1)} %pad_maximum_fusion.1), channel_id=1, replica_groups=mesh['dp'=4,'sp'=16] {'sp'}, use_global_device_ids=true, to_apply=%region_6.0 | all-reduce | flops 128 | bytes 1024 | tf_op jit(solution)/shard_map/psum | solution.py:22
  255.1 6.8 maximum_convert_fusion.6
  268.4 4.4 collective-permute-start.5
  280.3 5.2 collective-permute-done.6
  287.2 13.6 %fusion.125 = (f32[64]{0:T(128)S(1)}, f32[64]{0:T(128)S(1)}, f32[32,6,128,64]{3,0,2,1:T(8,128)}) fusion(bf16[6,3,3,64,64]{4,3,2,1,0:T(8,128)(2,1)} %param.12, bf16[32,1,128,64]{3,0,2,1:T(8,128)(2,1)S(1)} %copy.64, bf16[32,6,128,64]{3,0,2,1:T(8,128)(2,1)} %copy-done.2, bf16[32,1,128,64]{3,0,2,1:T(8,128)(2,1)S(1)} %copy.63), kind=kOutput, calls=%fused_computation.185 | convolution fusion | flops 1819803648 | bytes 13779456 | tf_op jit(solution)/shard_map/conv_general_dilated | solution.py:34
  300.8 25.5 %psum.72 = f32[2,64]{1,0:T(2,128)S(1)} all-reduce(f32[2,64]{1,0:T(2,128)S(1)} %pad_maximum_fusion.2), channel_id=1, replica_groups=mesh['dp'=4,'sp'=16] {'sp'}, use_global_device_ids=true, to_apply=%region_9.0 | all-reduce | flops 128 | bytes 1024 | tf_op jit(solution)/shard_map/psum | solution.py:22
  326.2 6.8 maximum_convert_fusion.5
  339.5 4.2 collective-permute-start.7
  351.5 5.1 collective-permute-done.8
  358.2 13.6 %fusion.124 = (f32[64]{0:T(128)S(1)}, f32[64]{0:T(128)S(1)}, f32[32,6,128,64]{3,0,2,1:T(8,128)}) fusion(bf16[6,3,3,64,64]{4,3,2,1,0:T(8,128)(2,1)} %param.12, bf16[32,1,128,64]{3,0,2,1:T(8,128)(2,1)S(1)} %copy.68, bf16[32,6,128,64]{3,0,2,1:T(8,128)(2,1)} %copy-done.3, bf16[32,1,128,64]{3,0,2,1:T(8,128)(2,1)S(1)} %copy.67), kind=kOutput, calls=%fused_computation.184 | convolution fusion | flops 1819803648 | bytes 13779456 | tf_op jit(solution)/shard_map/conv_general_dilated | solution.py:34
  371.8 25.5 %psum.73 = f32[2,64]{1,0:T(2,128)S(1)} all-reduce(f32[2,64]{1,0:T(2,128)S(1)} %pad_maximum_fusion.3), channel_id=1, replica_groups=mesh['dp'=4,'sp'=16] {'sp'}, use_global_device_ids=true, to_apply=%region_12.0 | all-reduce | flops 128 | bytes 1024 | tf_op jit(solution)/shard_map/psum | solution.py:22
  397.2 6.8 maximum_convert_fusion.4
  410.5 4.4 collective-permute-start.9
  422.5 5.2 collective-permute-done.10
  429.3 13.6 %fusion.123 = (f32[64]{0:T(128)S(1)}, f32[64]{0:T(128)S(1)}, f32[32,6,128,64]{3,0,2,1:T(8,128)}) fusion(bf16[6,3,3,64,64]{4,3,2,1,0:T(8,128)(2,1)} %param.12, bf16[32,1,128,64]{3,0,2,1:T(8,128)(2,1)S(1)} %copy.72, bf16[32,6,128,64]{3,0,2,1:T(8,128)(2,1)} %copy-done.4, bf16[32,1,128,64]{3,0,2,1:T(8,128)(2,1)S(1)} %copy.71), kind=kOutput, calls=%fused_computation.183 | convolution fusion | flops 1819803648 | bytes 13779456 | tf_op jit(solution)/shard_map/conv_general_dilated | solution.py:34
  442.9 25.5 %psum.74 = f32[2,64]{1,0:T(2,128)S(1)} all-reduce(f32[2,64]{1,0:T(2,128)S(1)} %pad_maximum_fusion.4), channel_id=1, replica_groups=mesh['dp'=4,'sp'=16] {'sp'}, use_global_device_ids=true, to_apply=%region_15.0 | all-reduce | flops 128 | bytes 1024 | tf_op jit(solution)/shard_map/psum | solution.py:22
  468.4 6.8 maximum_convert_fusion.3
  481.7 4.2 collective-permute-start.11
  493.6 5.1 collective-permute-done.12
  500.3 13.6 %fusion.122 = (f32[64]{0:T(128)S(1)}, f32[64]{0:T(128)S(1)}, f32[32,6,128,64]{3,0,2,1:T(8,128)}) fusion(bf16[6,3,3,64,64]{4,3,2,1,0:T(8,128)(2,1)} %param.12, bf16[32,1,128,64]{3,0,2,1:T(8,128)(2,1)S(1)} %copy.76, bf16[32,6,128,64]{3,0,2,1:T(8,128)(2,1)} %copy-done.5, bf16[32,1,128,64]{3,0,2,1:T(8,128)(2,1)S(1)} %copy.75), kind=kOutput, calls=%fused_computation.182 | convolution fusion | flops 1819803648 | bytes 13779456 | tf_op jit(solution)/shard_map/conv_general_dilated | solution.py:34
  513.9 25.5 %psum.75 = f32[2,64]{1,0:T(2,128)S(1)} all-reduce(f32[2,64]{1,0:T(2,128)S(1)} %pad_maximum_fusion.5), channel_id=1, replica_groups=mesh['dp'=4,'sp'=16] {'sp'}, use_global_device_ids=true, to_apply=%region_18.0 | all-reduce | flops 128 | bytes 1024 | tf_op jit(solution)/shard_map/psum | solution.py:22
  539.4 6.8 maximum_convert_fusion.2
  552.7 4.4 collective-permute-start.13
  564.6 5.2 collective-permute-done.14
  571.5 13.6 %fusion.121 = (f32[64]{0:T(128)S(1)}, f32[64]{0:T(128)S(1)}, f32[32,6,128,64]{3,0,2,1:T(8,128)}) fusion(bf16[6,3,3,64,64]{4,3,2,1,0:T(8,128)(2,1)} %param.12, bf16[32,1,128,64]{3,0,2,1:T(8,128)(2,1)S(1)} %copy.80, bf16[32,6,128,64]{3,0,2,1:T(8,128)(2,1)} %copy-done.6, bf16[32,1,128,64]{3,0,2,1:T(8,128)(2,1)S(1)} %copy.79), kind=kOutput, calls=%fused_computation.181 | convolution fusion | flops 1819803648 | bytes 13779456 | tf_op jit(solution)/shard_map/conv_general_dilated | solution.py:34
  585.1 25.5 %psum.76 = f32[2,64]{1,0:T(2,128)S(1)} all-reduce(f32[2,64]{1,0:T(2,128)S(1)} %pad_maximum_fusion.6), channel_id=1, replica_groups=mesh['dp'=4,'sp'=16] {'sp'}, use_global_device_ids=true, to_apply=%region_21.0 | all-reduce | flops 128 | bytes 1024 | tf_op jit(solution)/shard_map/psum | solution.py:22
  610.6 6.7 maximum_convert_fusion.1
  623.3 4.4 collective-permute-start.15
  627.8 6.1 collective-permute-done.15
  636.3 6.3 fusion.129
  642.6 25.2 %psum.77 = f32[2,128]{1,0:T(2,128)S(1)} all-reduce(f32[2,128]{1,0:T(2,128)S(1)} %pad_maximum_fusion.7), channel_id=1, replica_groups=mesh['dp'=4,'sp'=16] {'sp'}, use_global_device_ids=true, to_apply=%region_24.0 | all-reduce | flops 256 | bytes 2048 | tf_op jit(solution)/shard_map/psum | solution.py:22
  668.5 4.6 collective-permute-start.16
  679.1 4.4 collective-permute-done.17
  683.6 4.9 fusion.128
  688.5 25.0 %psum.78 = f32[2,128]{1,0:T(2,128)S(1)} all-reduce(f32[2,128]{1,0:T(2,128)S(1)} %pad_maximum_fusion.8), channel_id=1, replica_groups=mesh['dp'=4,'sp'=16] {'sp'}, use_global_device_ids=true, to_apply=%region_27.0 | all-reduce | flops 256 | bytes 2048 | tf_op jit(solution)/shard_map/psum | solution.py:22
  714.1 4.2 collective-permute-start.18
  724.4 4.4 collective-permute-done.19
  728.9 4.9 fusion.127
  733.8 25.5 %psum.79 = f32[2,128]{1,0:T(2,128)S(1)} all-reduce(f32[2,128]{1,0:T(2,128)S(1)} %pad_maximum_fusion.9), channel_id=1, replica_groups=mesh['dp'=4,'sp'=16] {'sp'}, use_global_device_ids=true, to_apply=%region_30.0 | all-reduce | flops 256 | bytes 2048 | tf_op jit(solution)/shard_map/psum | solution.py:22
  (135 shorter events, 137.7 us)
Async XLA Ops:
  0.0 636.3 %copy-start = (bf16[3,3,64,128]{3,2,1,0:T(8,128)(2,1)S(1)}, bf16[3,3,64,128]{3,2,1,0:T(8,128)(2,1)}, u32[]{:S(2)}) copy-start(bf16[3,3,64,128]{3,2,1,0:T(8,128)(2,1)} %param.14) | copy-start | bytes 442372
  1.4 22.6 %copy-start.12 = (f32[2,64]{1,0:T(2,128)S(1)}, f32[2,64]{1,0:T(2,128)}, u32[]{:S(2)}) copy-start(f32[2,64]{1,0:T(2,128)} %param.11) | copy-start | bytes 1540
  1.5 23.8 %collective-permute-start = (bf16[32,3,512,3]{2,0,3,1:T(8,128)(2,1)S(1)}, bf16[32,3,512,3]{2,0,3,1:T(8,128)(2,1)S(1)}, u32[]{:S(2)}, u32[]{:S(2)}) collective-permute-start(bf16[32,3,512,3]{2,0,3,1:T(8,128)(2,1)S(1)} %copy.84), channel_id=1, source_target_pairs={{0,1},{1,2},{2,3},{3,4},{4,5},{5,6},{6,7},{7,8},{8,9},{9,10},{10,1... | collective-permute-start | bytes 884744 | tf_op jit(solution)/shard_map/ppermute | solution.py:13
  7.8 18.4 %copy-start.15 = (bf16[7,7,3,64]{3,1,2,0:T(8,128)(2,1)S(1)}, bf16[7,7,3,64]{3,1,2,0:T(8,128)(2,1)}, u32[]{:S(2)}) copy-start(bf16[7,7,3,64]{3,1,2,0:T(8,128)(2,1)} %param.10) | copy-start | bytes 56452
  7.9 16.7 %collective-permute-start.1 = (bf16[32,2,512,3]{2,0,3,1:T(8,128)(2,1)S(1)}, bf16[32,2,512,3]{2,0,3,1:T(8,128)(2,1)S(1)}, u32[]{:S(2)}, u32[]{:S(2)}) collective-permute-start(bf16[32,2,512,3]{2,0,3,1:T(8,128)(2,1)S(1)} %copy.85), channel_id=1, source_target_pairs={{1,0},{2,1},{3,2},{4,3},{5,4},{6,5},{7,6},{8,7},{9,8},{10,9},{11,1... | collective-permute-start | bytes 589832 | tf_op jit(solution)/shard_map/ppermute | solution.py:16
  26.3 110.1 %copy-start.13 = (f32[2,64]{1,0:T(2,128)S(1)}, f32[2,64]{1,0:T(2,128)}, u32[]{:S(2)}) copy-start(f32[2,64]{1,0:T(2,128)} %param.11) | copy-start | bytes 1540
  26.3 110.1 %copy-start.11 = (f32[64]{0:T(128)S(1)}, f32[64]{0:T(128)}, u32[]{:S(2)}) copy-start(f32[64]{0:T(128)} %slice_bitcast_fusion.9) | copy-start | bytes 772
  168.1 13.7 %collective-permute-start.2 = (bf16[32,1,256,64]{2,3,1,0:T(8,128)(2,1)S(1)}, bf16[32,1,256,64]{2,3,1,0:T(8,128)(2,1)}, u32[]{:S(2)}, u32[]{:S(2)}) collective-permute-start(bf16[32,1,256,64]{2,3,1,0:T(8,128)(2,1)S(1)} %copy.55), channel_id=1, source_target_pairs={{0,1},{1,2},{2,3},{3,4},{4,5},{5,6},{6,7},{7,8},{8,9},{9,10},{10,1... | collective-permute-start | bytes 3145736 | tf_op jit(solution)/shard_map/ppermute | solution.py:13
  185.6 24.0 %copy-start.8 = (f32[6,2,64]{2,1,0:T(2,128)S(1)}, f32[6,2,64]{2,1,0:T(2,128)}, u32[]{:S(2)}) copy-start(f32[6,2,64]{2,1,0:T(2,128)} %param.13) | copy-start | bytes 9220
  197.6 2.6 copy-start.1
  201.7 10.5 %collective-permute-start.3 = (bf16[32,1,128,64]{2,3,1,0:T(8,128)(2,1)S(1)}, bf16[32,1,128,64]{2,3,1,0:T(8,128)(2,1)S(1)}, u32[]{:S(2)}, u32[]{:S(2)}) collective-permute-start(bf16[32,1,128,64]{2,3,1,0:T(8,128)(2,1)S(1)} %copy.57), channel_id=1, source_target_pairs={{0,1},{1,2},{2,3},{3,4},{4,5},{5,6},{6,7},{7,8},{8,9},{9,10},{10,1... | collective-permute-start | bytes 1572872 | tf_op jit(solution)/shard_map/ppermute | solution.py:13
  207.3 10.5 %collective-permute-start.4 = (bf16[32,1,128,64]{2,3,1,0:T(8,128)(2,1)S(1)}, bf16[32,1,128,64]{2,3,1,0:T(8,128)(2,1)S(1)}, u32[]{:S(2)}, u32[]{:S(2)}) collective-permute-start(bf16[32,1,128,64]{2,3,1,0:T(8,128)(2,1)S(1)} %copy.58), channel_id=1, source_target_pairs={{1,0},{2,1},{3,2},{4,3},{5,4},{6,5},{7,6},{8,7},{9,8},{10,9},{11,1... | collective-permute-start | bytes 1572872 | tf_op jit(solution)/shard_map/ppermute | solution.py:16
  261.8 2.6 copy-start.2
  268.4 10.3 %collective-permute-start.5 = (bf16[32,1,128,64]{2,3,1,0:T(8,128)(2,1)S(1)}, bf16[32,1,128,64]{2,3,1,0:T(8,128)(2,1)S(1)}, u32[]{:S(2)}, u32[]{:S(2)}) collective-permute-start(bf16[32,1,128,64]{2,3,1,0:T(8,128)(2,1)S(1)} %copy.61), channel_id=1, source_target_pairs={{0,1},{1,2},{2,3},{3,4},{4,5},{5,6},{6,7},{7,8},{8,9},{9,10},{10,1... | collective-permute-start | bytes 1572872 | tf_op jit(solution)/shard_map/ppermute | solution.py:13
  275.0 10.5 %collective-permute-start.6 = (bf16[32,1,128,64]{2,3,1,0:T(8,128)(2,1)S(1)}, bf16[32,1,128,64]{2,3,1,0:T(8,128)(2,1)S(1)}, u32[]{:S(2)}, u32[]{:S(2)}) collective-permute-start(bf16[32,1,128,64]{2,3,1,0:T(8,128)(2,1)S(1)} %copy.62), channel_id=1, source_target_pairs={{1,0},{2,1},{3,2},{4,3},{5,4},{6,5},{7,6},{8,7},{9,8},{10,9},{11,1... | collective-permute-start | bytes 1572872 | tf_op jit(solution)/shard_map/ppermute | solution.py:16
  333.0 2.6 copy-start.3
  339.5 10.3 %collective-permute-start.7 = (bf16[32,1,128,64]{2,3,1,0:T(8,128)(2,1)S(1)}, bf16[32,1,128,64]{2,3,1,0:T(8,128)(2,1)S(1)}, u32[]{:S(2)}, u32[]{:S(2)}) collective-permute-start(bf16[32,1,128,64]{2,3,1,0:T(8,128)(2,1)S(1)} %copy.65), channel_id=1, source_target_pairs={{0,1},{1,2},{2,3},{3,4},{4,5},{5,6},{6,7},{7,8},{8,9},{9,10},{10,1... | collective-permute-start | bytes 1572872 | tf_op jit(solution)/shard_map/ppermute | solution.py:13
  346.0 10.5 %collective-permute-start.8 = (bf16[32,1,128,64]{2,3,1,0:T(8,128)(2,1)S(1)}, bf16[32,1,128,64]{2,3,1,0:T(8,128)(2,1)S(1)}, u32[]{:S(2)}, u32[]{:S(2)}) collective-permute-start(bf16[32,1,128,64]{2,3,1,0:T(8,128)(2,1)S(1)} %copy.66), channel_id=1, source_target_pairs={{1,0},{2,1},{3,2},{4,3},{5,4},{6,5},{7,6},{8,7},{9,8},{10,9},{11,1... | collective-permute-start | bytes 1572872 | tf_op jit(solution)/shard_map/ppermute | solution.py:16
  404.0 2.6 copy-start.4
  410.5 10.3 %collective-permute-start.9 = (bf16[32,1,128,64]{2,3,1,0:T(8,128)(2,1)S(1)}, bf16[32,1,128,64]{2,3,1,0:T(8,128)(2,1)S(1)}, u32[]{:S(2)}, u32[]{:S(2)}) collective-permute-start(bf16[32,1,128,64]{2,3,1,0:T(8,128)(2,1)S(1)} %copy.69), channel_id=1, source_target_pairs={{0,1},{1,2},{2,3},{3,4},{4,5},{5,6},{6,7},{7,8},{8,9},{9,10},{10,1... | collective-permute-start | bytes 1572872 | tf_op jit(solution)/shard_map/ppermute | solution.py:13
  417.2 10.5 %collective-permute-start.10 = (bf16[32,1,128,64]{2,3,1,0:T(8,128)(2,1)S(1)}, bf16[32,1,128,64]{2,3,1,0:T(8,128)(2,1)S(1)}, u32[]{:S(2)}, u32[]{:S(2)}) collective-permute-start(bf16[32,1,128,64]{2,3,1,0:T(8,128)(2,1)S(1)} %copy.70), channel_id=1, source_target_pairs={{1,0},{2,1},{3,2},{4,3},{5,4},{6,5},{7,6},{8,7},{9,8},{10,9},{11,1... | collective-permute-start | bytes 1572872 | tf_op jit(solution)/shard_map/ppermute | solution.py:16
  475.2 2.6 copy-start.5
  481.7 10.3 %collective-permute-start.11 = (bf16[32,1,128,64]{2,3,1,0:T(8,128)(2,1)S(1)}, bf16[32,1,128,64]{2,3,1,0:T(8,128)(2,1)S(1)}, u32[]{:S(2)}, u32[]{:S(2)}) collective-permute-start(bf16[32,1,128,64]{2,3,1,0:T(8,128)(2,1)S(1)} %copy.73), channel_id=1, source_target_pairs={{0,1},{1,2},{2,3},{3,4},{4,5},{5,6},{6,7},{7,8},{8,9},{9,10},{10,1... | collective-permute-start | bytes 1572872 | tf_op jit(solution)/shard_map/ppermute | solution.py:13
  488.2 10.5 %collective-permute-start.12 = (bf16[32,1,128,64]{2,3,1,0:T(8,128)(2,1)S(1)}, bf16[32,1,128,64]{2,3,1,0:T(8,128)(2,1)S(1)}, u32[]{:S(2)}, u32[]{:S(2)}) collective-permute-start(bf16[32,1,128,64]{2,3,1,0:T(8,128)(2,1)S(1)} %copy.74), channel_id=1, source_target_pairs={{1,0},{2,1},{3,2},{4,3},{5,4},{6,5},{7,6},{8,7},{9,8},{10,9},{11,1... | collective-permute-start | bytes 1572872 | tf_op jit(solution)/shard_map/ppermute | solution.py:16
  546.2 2.6 copy-start.6
  552.7 10.3 %collective-permute-start.13 = (bf16[32,1,128,64]{2,3,1,0:T(8,128)(2,1)S(1)}, bf16[32,1,128,64]{2,3,1,0:T(8,128)(2,1)S(1)}, u32[]{:S(2)}, u32[]{:S(2)}) collective-permute-start(bf16[32,1,128,64]{2,3,1,0:T(8,128)(2,1)S(1)} %copy.77), channel_id=1, source_target_pairs={{0,1},{1,2},{2,3},{3,4},{4,5},{5,6},{6,7},{7,8},{8,9},{9,10},{10,1... | collective-permute-start | bytes 1572872 | tf_op jit(solution)/shard_map/ppermute | solution.py:13
  559.3 10.5 %collective-permute-start.14 = (bf16[32,1,128,64]{2,3,1,0:T(8,128)(2,1)S(1)}, bf16[32,1,128,64]{2,3,1,0:T(8,128)(2,1)S(1)}, u32[]{:S(2)}, u32[]{:S(2)}) collective-permute-start(bf16[32,1,128,64]{2,3,1,0:T(8,128)(2,1)S(1)} %copy.78), channel_id=1, source_target_pairs={{1,0},{2,1},{3,2},{4,3},{5,4},{6,5},{7,6},{8,7},{9,8},{10,9},{11,1... | collective-permute-start | bytes 1572872 | tf_op jit(solution)/shard_map/ppermute | solution.py:16
  571.5 39.1 %copy-start.9 = (f32[64]{0:T(128)S(1)}, f32[64]{0:T(128)}, u32[]{:S(2)}) copy-start(f32[64]{0:T(128)} %get-tuple-element.41) | copy-start | bytes 772
  610.6 17.1 %copy-start.14 = (f32[2,128]{1,0:T(2,128)S(1)}, f32[2,128]{1,0:T(2,128)}, u32[]{:S(2)}) copy-start(f32[2,128]{1,0:T(2,128)} %param.15) | copy-start | bytes 3076
  617.4 2.7 copy-start.7
  623.3 10.5 %collective-permute-start.15 = (bf16[32,1,128,64]{2,3,1,0:T(8,128)(2,1)S(1)}, bf16[32,1,128,64]{2,3,1,0:T(8,128)(2,1)S(1)}, u32[]{:S(2)}, u32[]{:S(2)}) collective-permute-start(bf16[32,1,128,64]{2,3,1,0:T(8,128)(2,1)S(1)} %copy.81), channel_id=1, source_target_pairs={{0,1},{1,2},{2,3},{3,4},{4,5},{5,6},{6,7},{7,8},{8,9},{9,10},{10,1... | collective-permute-start | bytes 1572872 | tf_op jit(solution)/shard_map/ppermute | solution.py:13
  636.3 38.7 %copy-start.10 = (f32[2,2,128]{2,1,0:T(2,128)S(1)}, f32[2,2,128]{2,1,0:T(2,128)}, u32[]{:S(2)}) copy-start(f32[2,2,128]{2,1,0:T(2,128)} %param.17) | copy-start | bytes 6148
  668.5 10.7 %collective-permute-start.16 = (bf16[32,1,64,128]{3,0,2,1:T(8,128)(2,1)S(1)}, bf16[32,1,64,128]{3,0,2,1:T(8,128)(2,1)S(1)}, u32[]{:S(2)}, u32[]{:S(2)}) collective-permute-start(bf16[32,1,64,128]{3,0,2,1:T(8,128)(2,1)S(1)} %get-tuple-element.39), channel_id=1, source_target_pairs={{0,1},{1,2},{2,3},{3,4},{4,5},{5,6},{6,7},{7,8},{8,9},{9,10},{10,1... | collective-permute-start | bytes 1572872 | tf_op jit(solution)/shard_map/ppermute | solution.py:13
  673.0 10.5 %collective-permute-start.17 = (bf16[32,1,64,128]{3,0,2,1:T(8,128)(2,1)S(1)}, bf16[32,1,64,128]{3,0,2,1:T(8,128)(2,1)S(1)}, u32[]{:S(2)}, u32[]{:S(2)}) collective-permute-start(bf16[32,1,64,128]{3,0,2,1:T(8,128)(2,1)S(1)} %get-tuple-element.40), channel_id=1, source_target_pairs={{1,0},{2,1},{3,2},{4,3},{5,4},{6,5},{7,6},{8,7},{9,8},{10,9},{11,1... | collective-permute-start | bytes 1572872 | tf_op jit(solution)/shard_map/ppermute | solution.py:16
  714.1 10.3 %collective-permute-start.18 = (bf16[32,1,64,128]{3,0,2,1:T(8,128)(2,1)S(1)}, bf16[32,1,64,128]{3,0,2,1:T(8,128)(2,1)S(1)}, u32[]{:S(2)}, u32[]{:S(2)}) collective-permute-start(bf16[32,1,64,128]{3,0,2,1:T(8,128)(2,1)S(1)} %get-tuple-element.37), channel_id=1, source_target_pairs={{0,1},{1,2},{2,3},{3,4},{4,5},{5,6},{6,7},{7,8},{8,9},{9,10},{10,1... | collective-permute-start | bytes 1572872 | tf_op jit(solution)/shard_map/ppermute | solution.py:13
  718.4 10.5 %collective-permute-start.19 = (bf16[32,1,64,128]{3,0,2,1:T(8,128)(2,1)S(1)}, bf16[32,1,64,128]{3,0,2,1:T(8,128)(2,1)S(1)}, u32[]{:S(2)}, u32[]{:S(2)}) collective-permute-start(bf16[32,1,64,128]{3,0,2,1:T(8,128)(2,1)S(1)} %get-tuple-element.38), channel_id=1, source_target_pairs={{1,0},{2,1},{3,2},{4,3},{5,4},{6,5},{7,6},{8,7},{9,8},{10,9},{11,1... | collective-permute-start | bytes 1572872 | tf_op jit(solution)/shard_map/ppermute | solution.py:16
where the time goes:
time: 776 us; the launch traced here: 762 us
  blocking collectives  252 us (32%)
  matrix products  181 us (23%)
  local copies, waits for them, and re-layouts  105 us (14%)
  other arithmetic  82.4 us (11%)
  waiting for transfers between devices  74.5 us (10%)
  starting transfers between devices  66.2 us (9%)
    psum x10, blocking collectives, norm_relu(): totals = lax.psum(local_sums, 'sp')  252 us
    conv_general_dilated x10, matrix products, conv_layer(): lax.conv_general_dilated(halo_rows(hidden, above, below, group), kernel,...  181 us
    convert_element_type x10, other arithmetic, norm_relu(): jnp.maximum((conv_out - ch_mean) * ch_scale + bn_pair[1], 0.0)  70.1 us
    ppermute x11, starting transfers between devices, halo_rows(): lax.ppermute(tile[:, -above:], 'sp', [(i, i + 1) for i in range(group - 1)])  46.3 us
    ppermute x9, waiting for transfers between devices, halo_rows(): lax.ppermute(tile[:, :below], 'sp', [(i + 1, i) for i in range(group - 1)])  38.7 us
    ppermute x11, waiting for transfers between devices, halo_rows(): lax.ppermute(tile[:, -above:], 'sp', [(i, i + 1) for i in range(group - 1)])  35.9 us
    unnamed x35, local copies, waits for them, and re-layouts  31.8 us
    slice x19, local copies, waits for them, and re-layouts, halo_rows(): tile[:, -above:]  29.6 us
  transfers between devices with their start and end apart: 20, of which 18 were waited for; matrix products, arithmetic and copies ran while one was open for 5% of the time, Pallas kernels for 0%

commit v1 on v0

v1 whole, which is shorter than its diff:
```python
import functools

import jax
import jax.numpy as jnp
from jax import lax
from jax.experimental import pallas as pl
from jax.experimental.pallas import tpu as pltpu
from jax.sharding import PartitionSpec as P

BN_EPS = 1e-5
F32 = jnp.float32
BF16 = jnp.bfloat16


def half_swap(x):
    return pltpu.roll(x, 64, x.ndim - 1)


def low_half(shape):
    return lax.broadcasted_iota(jnp.int32, shape, len(shape) - 1) < 64


def whole_kernel(group, counts, xk_ref, ws_ref, wa_ref, wd_ref, wb_ref, bns_ref, bna_ref, bnd_ref, bnb_ref, out_ref,
                 zs, za, ya, hb, yb, wat, wdt, acc, slots, ssend, srecv, hsend, hrecv):
    me = lax.axis_index("sp")
    nimg = za.shape[2]
    rows = za.shape[0]
    cols = za.shape[1]
    srows = zs.shape[0]
    orows = out_ref.shape[0]
    layers = wa_ref.shape[0]
    cnt_s, cnt_a, cnt_b = counts
    up, down = me - 1, me + 1

    barrier = pltpu.get_barrier_semaphore()
    for k in range(1, group):
        pl.semaphore_signal(barrier, inc=1, device_id={"sp": lax.rem(me + k, group)})

    def zero_rows(ref):
        @pl.loop(0, ref.shape[0])
        def _(r):
            ref[r] = jnp.zeros(ref.shape[1:], ref.dtype)

    zero_rows(ya)
    zero_rows(yb)
    hb[0] = jnp.zeros(hb.shape[1:], hb.dtype)

    @pl.loop(0, layers)
    def _(l):
        for r in range(4):
            for slot, t in enumerate((1, 2, 3, 0)):
                for dy in range(2):
                    ky = r - dy
                    parts = []
                    for dx in range(2):
                        kx = t - dx
                        if 0 <= ky < 3 and 0 <= kx < 3:
                            parts.append(wa_ref[l, ky, kx])
                        else:
                            parts.append(jnp.zeros((64, 64), BF16))
                    wat[l, pl.ds(r * 256 + slot * 64, 64), pl.ds(dy * 128, 128)] = jnp.concatenate(parts, axis=1)

    for r in range(3):
        for slot, kx in enumerate((1, 2, None, 0)):
            wdt[pl.ds(r * 256 + slot * 64, 64), :] = jnp.zeros((64, 128), BF16) if kx is None else wd_ref[r, kx]

    def clear_acc():
        acc[...] = jnp.zeros_like(acc)

    def add_acc(parts):
        s, q = acc[0], acc[1]
        for z in parts:
            z3 = z.reshape(z.shape[0] // 8, 8, z.shape[1])
            s = s + jnp.sum(z3, axis=0)
            q = q + jnp.sum(z3 * z3, axis=0)
        acc[0] = s
        acc[1] = q

    def stat_copy(par, k, source):
        block = slots.at[par, source]
        return pltpu.make_async_remote_copy(
            src_ref=block, dst_ref=block, send_sem=ssend.at[par, k], recv_sem=srecv.at[par, k],
            device_id={"sp": lax.rem(me + k, group)})

    def reduce_stats(par, bn, count, fold):
        s = jnp.sum(acc[0], axis=0, keepdims=True)
        q = jnp.sum(acc[1], axis=0, keepdims=True)
        slots[par, me] = jnp.concatenate([s, q, jnp.zeros((6, 128), F32)], axis=0)
        for k in range(1, group):
            stat_copy(par, k, me).start()
        for k in range(1, group):
            stat_copy(par, k, lax.rem(me + group - k, group)).wait_recv()
        for k in range(1, group):
            stat_copy(par, k, me).wait_send()
        total = slots[par, 0]
        for d in range(1, group):
            total = total + slots[par, d]
        if fold:
            total = total + half_swap(total)
        mean = total[0:1] / count
        var = total[1:2] / count - mean * mean
        scale = bn[0:1] * lax.rsqrt(var + BN_EPS)
        return mean, scale, bn[1:2]

    def apply(z, coef):
        mean, scale, beta = coef
        return jnp.maximum((z - mean) * scale + beta, 0.0)

    def send_up(buf, row, halo):
        return pltpu.make_async_remote_copy(
            src_ref=buf.at[row], dst_ref=buf.at[halo], send_sem=hsend.at[0], recv_sem=hrecv.at[0],
            device_id={"sp": up})

    def send_down(buf, row, halo):
        return pltpu.make_async_remote_copy(
            src_ref=buf.at[row], dst_ref=buf.at[halo], send_sem=hsend.at[1], recv_sem=hrecv.at[1],
            device_id={"sp": down})

    has_up, has_down = me > 0, me < group - 1

    def start_halos(buf, n):
        @pl.when(has_up)
        def _():
            send_up(buf, 1, n + 1).start()

        @pl.when(has_down)
        def _():
            send_down(buf, n, 0).start()

    def wait_halos(buf, n):
        @pl.when(has_up)
        def _():
            send_down(buf, n, 0).wait_recv()

        @pl.when(has_down)
        def _():
            send_up(buf, 1, n + 1).wait_recv()

    def drain_halos(buf, n):
        @pl.when(has_up)
        def _():
            send_up(buf, 1, n + 1).wait_send()

        @pl.when(has_down)
        def _():
            send_down(buf, n, 0).wait_send()

    clear_acc()
    pairs = srows + 3
    lanes = lax.broadcasted_iota(jnp.int32, (pairs, nimg, 128), 2)

    @pl.loop(0, xk_ref.shape[0])
    def _(kk):
        for jj in range(8):
            packed = None
            for r in range(2):
                for c in range(3):
                    off = r * 64 + c * 16
                    piece = xk_ref[kk, c, r]
                    shift = (off - 8 * jj) % 128
                    if shift:
                        piece = pltpu.roll(piece, shift, 2)
                    packed = piece if packed is None else jnp.where(lanes < off, packed, piece)
            lhs = jnp.concatenate([packed[p:p + srows].reshape(srows * nimg, 128) for p in range(4)], axis=1)
            z = jnp.dot(lhs, ws_ref[...], preferred_element_type=F32)
            j = kk * 8 + jj
            zl, zh = z[:, :128], z[:, 128:]
            zs[:, 0, pl.ds(j + 1, 1)] = zl.reshape(srows, 1, nimg, 128)
            zs[:, 1, pl.ds(j + 1, 1)] = zh.reshape(srows, 1, nimg, 128)
            add_acc([zl, zh])

    for h in range(srows):
        zs[h, 1, 0] = jnp.zeros((nimg, 128), F32)

    pl.semaphore_wait(barrier, group - 1)
    coef = reduce_stats(0, bns_ref[...], cnt_s, True)

    jp = 8

    def pool_row(h, jb):
        a = apply(zs[h, 0, pl.ds(jb * jp + 1, jp)], coef)
        b = apply(zs[h, 1, pl.ds(jb * jp, jp + 1)], coef)
        first = lax.broadcasted_iota(jnp.int32, b.shape, 0) + jb * jp
        b = jnp.where(first == 0, 0.0, b)
        rb = half_swap(b)
        lo = low_half(a.shape)
        m = jnp.maximum(a, jnp.where(lo, half_swap(a), rb[1:]))
        return jnp.maximum(m, jnp.where(lo, rb[:jp], b[1:]))

    def pool_pair(p):
        @pl.loop(0, cols // jp)
        def _(jb):
            top = pool_row(2 * p, jb)
            bot = pool_row(2 * p + 1, jb)
            hb[p + 1, pl.ds(jb * jp, jp)] = bot.astype(BF16)
            ya[p + 1, pl.ds(jb * jp + 1, jp)] = jnp.maximum(top, bot).astype(BF16)

    def pool_join(p):
        @pl.loop(0, cols // jp)
        def _(jb):
            old = ya[p + 1, pl.ds(jb * jp + 1, jp)]
            ya[p + 1, pl.ds(jb * jp + 1, jp)] = jnp.maximum(old, hb[p, pl.ds(jb * jp, jp)])

    pool_pair(rows - 1)

    def send_pool():
        return pltpu.make_async_remote_copy(
            src_ref=hb.at[rows], dst_ref=hb.at[0], send_sem=hsend.at[2], recv_sem=hrecv.at[2],
            device_id={"sp": down})

    @pl.when(has_down)
    def _():
        send_pool().start()

    @pl.loop(0, rows - 1)
    def _(p):
        pool_pair(p)

    @pl.loop(1, rows)
    def _(p):
        pool_join(p)

    @pl.when(has_up)
    def _():
        send_pool().wait_recv()

    pool_join(0)

    @pl.when(has_down)
    def _():
        send_pool().wait_send()

    start_halos(ya, rows)

    ja = 8

    def conv_a(l, i, jb):
        parts = []
        lo = low_half((ja, nimg, 128))
        for r in range(4):
            row = 2 * i + r
            mid = ya[row, pl.ds(jb * ja + 1, ja)]
            left = ya[row, pl.ds(jb * ja, ja)]
            right = ya[row, pl.ds(jb * ja + 2, ja)]
            parts.append(mid.reshape(ja * nimg, 128))
            parts.append(jnp.where(lo, right, left).reshape(ja * nimg, 128))
        z = jnp.dot(jnp.concatenate(parts, axis=1), wat[l], preferred_element_type=F32)
        for dy in range(2):
            za[2 * i + dy, pl.ds(jb * ja, ja)] = z[:, dy * 128:(dy + 1) * 128].reshape(ja, nimg, 128)
        add_acc([z[:, :128], z[:, 128:]])

    def norm_row(dst, row, coef):
        @pl.loop(0, cols // jp)
        def _(jb):
            dst[row + 1, pl.ds(jb * jp + 1, jp)] = apply(za[row, pl.ds(jb * jp, jp)], coef).astype(BF16)

    nblk = cols // ja

    @pl.loop(0, layers)
    def _(l):
        clear_acc()

        @pl.loop(0, (rows // 2 - 2) * nblk)
        def _(s):
            conv_a(l, 1 + lax.div(s, nblk), lax.rem(s, nblk))

        wait_halos(ya, rows)

        @pl.loop(0, 2 * nblk)
        def _(s):
            conv_a(l, lax.div(s, nblk) * (rows // 2 - 1), lax.rem(s, nblk))

        drain_halos(ya, rows)
        coef = reduce_stats(lax.rem(l + 1, 2), bna_ref[l], cnt_a, True)
        norm_row(ya, 0, coef)
        norm_row(ya, rows - 1, coef)
        start_halos(ya, rows)

        @pl.loop(1, rows - 1)
        def _(row):
            norm_row(ya, row, coef)

    clear_acc()
    jd = 16
    nblk_d = cols // jd

    def conv_d(i, jb):
        parts = []
        for r in range(3):
            row = 2 * i + r
            parts.append(ya[row, pl.ds(jb * jd + 1, jd)].reshape(jd * nimg, 128))
            parts.append(ya[row, pl.ds(jb * jd, jd)].reshape(jd * nimg, 128))
        z = jnp.dot(jnp.concatenate(parts, axis=1), wdt[...], preferred_element_type=F32)
        za[i, pl.ds(jb * jd, jd)] = z.reshape(jd, nimg, 128)
        add_acc([z])

    @pl.loop(0, (orows - 1) * nblk_d)
    def _(s):
        conv_d(1 + lax.div(s, nblk_d), lax.rem(s, nblk_d))

    wait_halos(ya, rows)

    @pl.loop(0, nblk_d)
    def _(jb):
        conv_d(0, jb)

    drain_halos(ya, rows)
    par = (layers + 1) % 2
    coef = reduce_stats(par, bnd_ref[...], cnt_b, False)

    def conv_b(l, i, jb):
        parts = []
        for r in range(3):
            for t in range(3):
                parts.append(yb[i + r, pl.ds(jb * jd + t, jd)].reshape(jd * nimg, 128))
        z = jnp.dot(jnp.concatenate(parts, axis=1), wb_ref[l], preferred_element_type=F32)
        za[i, pl.ds(jb * jd, jd)] = z.reshape(jd, nimg, 128)
        add_acc([z])

    for l in range(wb_ref.shape[0]):
        norm_row(yb, 0, coef)
        norm_row(yb, orows - 1, coef)
        start_halos(yb, orows)
        for row in range(1, orows - 1):
            norm_row(yb, row, coef)
        clear_acc()

        @pl.loop(0, (orows - 2) * nblk_d)
        def _(s):
            conv_b(l, 1 + lax.div(s, nblk_d), lax.rem(s, nblk_d))

        wait_halos(yb, orows)

        @pl.loop(0, 2 * nblk_d)
        def _(s):
            conv_b(l, lax.div(s, nblk_d) * (orows - 1), lax.rem(s, nblk_d))

        drain_halos(yb, orows)
        par = 1 - par
        coef = reduce_stats(par, bnb_ref[l], cnt_b, False)

    @pl.loop(0, orows)
    def _(row):
        @pl.loop(0, cols // jp)
        def _(jb):
            out_ref[row, pl.ds(jb * jp, jp)] = apply(za[row, pl.ds(jb * jp, jp)], coef).astype(BF16)


def stem_weights(w):
    w = jnp.pad(w, ((1, 0), (0, 0), (0, 1), (0, 0)))
    cols = [jnp.pad(w, ((0, 0), (2 * q + 1, 8 - 2 * q), (0, 0), (0, 0))) for q in range(4)]
    return jnp.concatenate(cols, axis=-1).transpose(0, 2, 1, 3).reshape(8 * 4 * 16, 256)


def solution(mesh):
    group = mesh.shape["sp"]

    def local_stack(pixels, w_stem, bn_stem, w_a, bn_a, w_down, bn_down, w_b, bn_b):
        n, h, w, chans = pixels.shape
        x = pixels.transpose(3, 1, 0, 2)
        above = lax.ppermute(x[:, -3:], "sp", [(i, i + 1) for i in range(group - 1)])
        below = lax.ppermute(x[:, :2], "sp", [(i + 1, i) for i in range(group - 1)])
        x = jnp.concatenate([jnp.zeros_like(x[:, :1]), above, x, below], axis=1)
        x = jnp.pad(x, ((0, 0), (0, 0), (0, 0), (4, 60)))
        hp = x.shape[1] // 2
        x = x.reshape(chans, hp, 2, n, (w + 64) // 64, 64).transpose(4, 0, 2, 1, 3, 5)
        xk = jnp.concatenate([x[:-1], x[1:]], axis=-1)
        rows, cols, orows = h // 4, w // 8, h // 8
        counts = (float(n * (h // 2) * group * (w // 2)), float(n * rows * group * (w // 4)), float(n * orows * group * (w // 8)))
        vm = pl.BlockSpec(memory_space=pltpu.VMEM)
        out = pl.pallas_call(
            functools.partial(whole_kernel, group, counts),
            out_shape=jax.ShapeDtypeStruct((orows, cols, n, 128), BF16),
            in_specs=[vm] * 9,
            out_specs=vm,
            scratch_shapes=[
                pltpu.VMEM((h // 2, 2, cols + 1, n, 128), F32),
                pltpu.VMEM((rows, cols, n, 128), F32),
                pltpu.VMEM((rows + 2, cols + 2, n, 128), BF16),
                pltpu.VMEM((rows + 1, cols, n, 128), BF16),
                pltpu.VMEM((orows + 2, cols + 2, n, 128), BF16),
                pltpu.VMEM((w_a.shape[0], 1024, 256), BF16),
                pltpu.VMEM((768, 128), BF16),
                pltpu.VMEM((2, 8, 128), F32),
                pltpu.VMEM((2, group, 8, 128), F32),
                pltpu.SemaphoreType.DMA((2, group)),
                pltpu.SemaphoreType.DMA((2, group)),
                pltpu.SemaphoreType.DMA((3,)),
                pltpu.SemaphoreType.DMA((3,)),
            ],
            compiler_params=pltpu.CompilerParams(collective_id=0, has_side_effects=True, vmem_limit_bytes=63 * 1024 * 1024),
        )(xk, stem_weights(w_stem), w_a, w_down, w_b.reshape(w_b.shape[0], 9 * 128, 128),
          jnp.tile(bn_stem, (1, 2)), jnp.tile(bn_a, (1, 1, 2)), bn_down, bn_b)
        return out.transpose(2, 0, 1, 3)

    return jax.shard_map(local_stack, mesh=mesh, in_specs=(P("dp", "sp"),) + (P(),) * 8, out_specs=P("dp", "sp"), check_vma=False)
```

time: 776 us -> 264 us (0.34); the launches traced: 762 us -> 263 us
  blocking collectives: 252 us -> 0 us
  Pallas kernels: 0 us -> 201 us
  matrix products: 181 us -> 0 us
  waiting for transfers between devices: 74.5 us -> 0.01 us
  other arithmetic: 82.4 us -> 14.8 us
  local copies, waits for them, and re-layouts: 105 us -> 38.7 us
  starting transfers between devices: 66.2 us -> 7.92 us
    psum x10 -> x0, blocking collectives: 252 us -> none  [norm_relu(): totals = lax.psum(local_sums, 'sp')]
    pallas_call x0 -> x1, Pallas kernels: none -> 201 us  [local_stack(): pl.pallas_call(functools.partial(whole_kernel, group, counts), out_shape=...]
    conv_general_dilated x10 -> x0, matrix products: 181 us -> none  [conv_layer(): lax.conv_general_dilated(halo_rows(hidden, above, below, group), kernel,...]
    ppermute x20 -> x2, waiting for transfers between devices: 74.5 us -> 0.01 us  [the longest x1 0.01 us: local_stack(): below = lax.ppermute(x[:, :2], 'sp', [(i + 1, i) for i in range(group - 1)])]
    convert_element_type x10 -> x0, other arithmetic: 70.1 us -> none  [norm_relu(): jnp.maximum((conv_out - ch_mean) * ch_scale + bn_pair[1], 0.0)]
    ppermute x20 -> x2, starting transfers between devices: 66.2 us -> 7.92 us  [the longest x1 5.1 us: local_stack(): lax.ppermute(x[:, -3:], 'sp', [(i, i + 1) for i in range(group - 1)])]
    slice x26 -> x3, local copies, waits for them, and re-layouts: 43.1 us -> 8.03 us  [the longest x1 5.45 us: local_stack(): xk = jnp.concatenate([x[:-1], x[1:]], axis=-1)]
    unnamed x35 -> x0, local copies, waits for them, and re-layouts: 31.8 us -> none
  transfers between devices with their start and end apart: 20 -> 2, of which waited for: 18 -> 0; matrix products, arithmetic and copies ran while one was open for 5% -> 2% of each run, Pallas kernels for 0% -> 0%
where the time goes in v1:
time: 264 us; the launch traced here: 263 us
  Pallas kernels  201 us (76%)
  local copies, waits for them, and re-layouts  38.7 us (15%)
  other arithmetic  14.8 us (6%)
  starting transfers between devices  7.92 us (3%)
    pallas_call x1, Pallas kernels, local_stack(): pl.pallas_call(functools.partial(whole_kernel, group, counts), out_shape=...  201 us
    reshape x2, local copies, waits for them, and re-layouts, local_stack(): x.reshape(chans, hp, 2, n, (w + 64) // 64, 64).transpose(4, 0, 2, 1, 3, 5)  19.9 us
    concatenate x1, other arithmetic, local_stack(): xk = jnp.concatenate([x[:-1], x[1:]], axis=-1)  10.1 us
    slice x1, local copies, waits for them, and re-layouts, local_stack(): xk = jnp.concatenate([x[:-1], x[1:]], axis=-1)  5.45 us
  transfers between devices with their start and end apart: 2, of which 0 were waited for; matrix products, arithmetic and copies ran while one was open for 2% of the time, Pallas kernels for 0%

profile of v1, /device:TPU:21, one launch (start us, length us, event | category | flops | bytes accessed | tf_op | source)
XLA Modules:
  0.0 263.0 jit_solution(17102197283965042784)
XLA Ops:
  0.0 1.3 slice.16
  1.3 5.1 %collective-permute-start = (bf16[3,3,32,512]{3,1,0,2:T(4,128)(2,1)S(1)}, bf16[3,3,32,512]{3,1,0,2:T(4,128)(2,1)S(1)}, u32[]{:S(2)}, u32[]{:S(2)}) collective-permute-start(bf16[3,3,32,512]{3,1,0,2:T(4,128)(2,1)S(1)} %slice.16), channel_id=1, source_target_pairs={{0,1},{1,2},{2,3},{3,4},{4,5},{5,6},{6,7},{7,8},{8,9},{9,10},{10,1... | collective-permute-start | bytes 884744 | tf_op jit(solution)/shard_map/ppermute | solution.py:361
  6.4 1.2 slice.17
  7.7 2.8 %collective-permute-start.1 = (bf16[3,2,32,512]{3,1,0,2:T(2,128)(2,1)S(1)}, bf16[3,2,32,512]{3,1,0,2:T(2,128)(2,1)S(1)}, u32[]{:S(2)}, u32[]{:S(2)}) collective-permute-start(bf16[3,2,32,512]{3,1,0,2:T(2,128)(2,1)S(1)} %slice.17), channel_id=1, source_target_pairs={{1,0},{2,1},{3,2},{4,3},{5,4},{6,5},{7,6},{8,7},{9,8},{10,9},{11,1... | collective-permute-start | bytes 589832 | tf_op jit(solution)/shard_map/ppermute | solution.py:362
  10.5 0.7 tile.20
  11.2 0.7 tile.21.bna_ref
  11.9 0.7 tile.8
  12.6 0.7 tile.9.bns_ref
  13.3 0.8 pad.25
  14.1 0.9 fusion.7
  15.0 0.0 collective-permute-done.1
  15.0 0.0 collective-permute-done
  15.0 3.7 %pad_maximum_fusion.1 = bf16[3,30,32,512]{3,1,0,2:T(8,128)(2,1)S(1)} fusion(bf16[3,2,32,512]{3,1,0,2:T(2,128)(2,1)S(1)} %collective-permute-done.1, bf16[3,24,32,512]{3,1,0,2:T(8,128)(2,1)} %bitcast.16, bf16[3,3,32,512]{3,1,0,2:T(4,128)(2,1)S(1)} %collective-permute-done, bf16[30]{0:T(256)(128)(2,1)S(1)} %pad.36.clone), kind=kLoop, calls=%fused_computation.2 | loop fusion | flops 11796480 | bytes 5799996 | tf_op jit(solution)/shard_map/concatenate | solution.py:363
  18.8 4.1 %pad.24 = bf16[3,30,32,576]{3,1,0,2:T(8,128)(2,1)} pad(bf16[3,30,32,512]{3,1,0,2:T(8,128)(2,1)S(1)} %pad_maximum_fusion.1, bf16[]{:T(256)} %constant.1.clone.1), padding=0_0x0_0x0_0x4_60 | pad | bytes 6266882 | tf_op jit(solution)/shard_map/jit(_pad)/pad | solution.py:364
  22.9 12.8 %reshape.20 = bf16[3,15,2,32,9,64]{5,4,2,1,0,3:T(8,128)(2,1)} reshape(bf16[3,30,32,576]{3,1,0,2:T(8,128)(2,1)} %pad.24) | data formatting | bytes 6635520 | tf_op jit(solution)/shard_map/reshape | solution.py:366
  35.6 7.1 %copy.17 = bf16[3,15,2,32,9,64]{5,3,1,2,0,4:T(8,128)(2,1)S(1)} copy(bf16[3,15,2,32,9,64]{5,4,2,1,0,3:T(8,128)(2,1)} %reshape.20) | data formatting | bytes 6635520 | tf_op jit(solution)/shard_map/reshape | solution.py:366
  42.7 5.5 %fusion.9 = (bf16[8,3,2,15,32,64]{5,4,3,2,1,0:T(8,128)(2,1)}, bf16[8,3,2,15,32,64]{5,4,3,2,1,0:T(8,128)(2,1)}) fusion(bf16[9,3,2,15,32,64]{5,4,3,2,1,0:T(8,128)(2,1)S(1)} %bitcast.12), kind=kLoop, calls=%fused_computation.18 | loop fusion | bytes 11796480 | tf_op jit(solution)/shard_map/slice | solution.py:367
  48.2 10.1 %pad_maximum_fusion.xk_ref = bf16[8,3,2,15,32,128]{5,4,3,2,1,0:T(8,128)(2,1)} fusion(bf16[8,3,2,15,32,64]{5,4,3,2,1,0:T(8,128)(2,1)} %get-tuple-element.6, bf16[8,3,2,15,32,64]{5,4,3,2,1,0:T(8,128)(2,1)} %get-tuple-element.5), kind=kLoop, calls=%fused_computation.1 | loop fusion | flops 11796480 | bytes 11796480 | tf_op jit(solution)/shard_map/concatenate | solution.py:367
  58.3 201.5 %shard_map.91 = bf16[3,64,32,128]{3,2,1,0:T(8,128)(2,1)} custom-call(bf16[8,3,2,15,32,128]{5,4,3,2,1,0:T(8,128)(2,1)} %pad_maximum_fusion.xk_ref, bf16[512,256]{1,0:T(8,128)(2,1)} %bitcast.17, bf16[6,3,3,64,64]{4,3,2,1,0:T(8,128)(2,1)} %wa_ref.1, bf16[3,3,64,128]{3,2,1,0:T(8,128)(2,1)} %wd_ref.1, bf16[2,1152,128]{2,1,0:T(8,128)(2,1)} %bitcast.18, ...), custom_call_target="tpu_custom_call" | custom-call | tf_op jit(solution)/shard_map/pallas_call | solution.py:371
  259.8 3.2 %copy.13 = bf16[32,3,64,128]{3,2,1,0:T(8,128)(2,1)} copy(bf16[32,3,64,128]{3,0,2,1:T(8,128)(2,1)} %bitcast.13) | data formatting | bytes 3145728 | tf_op jit(solution)/shard_map/transpose | solution.py:394
  (1 shorter events, 0.0 us)
Async XLA Ops:
  1.3 13.7 %collective-permute-start = (bf16[3,3,32,512]{3,1,0,2:T(4,128)(2,1)S(1)}, bf16[3,3,32,512]{3,1,0,2:T(4,128)(2,1)S(1)}, u32[]{:S(2)}, u32[]{:S(2)}) collective-permute-start(bf16[3,3,32,512]{3,1,0,2:T(4,128)(2,1)S(1)} %slice.16), channel_id=1, source_target_pairs={{0,1},{1,2},{2,3},{3,4},{4,5},{5,6},{6,7},{7,8},{8,9},{9,10},{10,1... | collective-permute-start | bytes 884744 | tf_op jit(solution)/shard_map/ppermute | solution.py:361
  7.7 7.3 %collective-permute-start.1 = (bf16[3,2,32,512]{3,1,0,2:T(2,128)(2,1)S(1)}, bf16[3,2,32,512]{3,1,0,2:T(2,128)(2,1)S(1)}, u32[]{:S(2)}, u32[]{:S(2)}) collective-permute-start(bf16[3,2,32,512]{3,1,0,2:T(2,128)(2,1)S(1)} %slice.17), channel_id=1, source_target_pairs={{1,0},{2,1},{3,2},{4,3},{5,4},{6,5},{7,6},{8,7},{9,8},{10,9},{11,1... | collective-permute-start | bytes 589832 | tf_op jit(solution)/shard_map/ppermute | solution.py:362

commit v2 on v1

v2 whole, which is shorter than its diff:
```python
import functools

import jax
import jax.numpy as jnp
from jax import lax
from jax.experimental import pallas as pl
from jax.experimental.pallas import tpu as pltpu
from jax.sharding import PartitionSpec as P

BN_EPS = 1e-5
F32 = jnp.float32
BF16 = jnp.bfloat16


def half_swap(x):
    return pltpu.roll(x, 64, x.ndim - 1)


def low_half(shape):
    return lax.broadcasted_iota(jnp.int32, shape, len(shape) - 1) < 64


def whole_kernel(group, counts, x_ref, w7_ref, wa_ref, wd_ref, wb_ref, bns_ref, bna_ref, bnd_ref, bnb_ref, out_ref,
                 xt, xw, zs, za, zr, ya, hb, yb, wtmp, ws, wat, wdt, acc, slots, ssend, srecv, hsend, hrecv, psend, precv, zsend, zrecv):
    me = lax.axis_index("sp")
    nimg = za.shape[2]
    rows = za.shape[0]
    cols = za.shape[1]
    chunks, xpairs = xt.shape[0], xt.shape[1]
    own = xpairs - 4
    srows = own + 1
    orows = out_ref.shape[1]
    layers = wa_ref.shape[0]
    chans = x_ref.shape[1]
    cnt_s, cnt_a, cnt_b = counts
    up, down = me - 1, me + 1
    has_up, has_down = me > 0, me < group - 1
    even = lax.rem(me, 2) == 0
    odd = jnp.logical_not(even)

    for m in range(chunks):
        xt[m, 0:3] = jnp.zeros((3,) + xt.shape[2:], BF16)
        xt[m, xpairs - 1] = jnp.zeros(xt.shape[2:], BF16)

    barrier = pltpu.get_barrier_semaphore()
    for k in range(1, group):
        pl.semaphore_signal(barrier, inc=1, device_id={"sp": lax.rem(me + k, group)})

    @pl.loop(0, chans)
    def _(c):
        for h in range(own // 4):
            v = x_ref[:, c, pl.ds(8 * h, 8), :].astype(F32)
            v = jnp.transpose(v, (1, 0, 2)).astype(BF16)
            for m in range(chunks):
                for g in range(4):
                    for r in range(2):
                        xt[m, 3 + 4 * h + g, r, c] = v[2 * g + r, :, m * 128:(m + 1) * 128]

    def pix_down(m):
        return pltpu.make_async_remote_copy(
            src_ref=xt.at[m, pl.ds(own, 3)], dst_ref=xt.at[m, pl.ds(0, 3)], send_sem=psend.at[0, m], recv_sem=precv.at[0, m],
            device_id={"sp": down})

    def pix_up(m):
        return pltpu.make_async_remote_copy(
            src_ref=xt.at[m, pl.ds(3, 1)], dst_ref=xt.at[m, pl.ds(own + 3, 1)], send_sem=psend.at[1, m], recv_sem=precv.at[1, m],
            device_id={"sp": up})

    pl.semaphore_wait(barrier, group - 1)

    @pl.when(has_down)
    def _():
        for m in range(chunks):
            pix_down(m).start()

    @pl.when(has_up)
    def _():
        for m in range(chunks):
            pix_up(m).start()

    def zero_rows(ref):
        @pl.loop(0, ref.shape[0])
        def _(r):
            ref[r] = jnp.zeros(ref.shape[1:], ref.dtype)

    zero_rows(ya)
    zero_rows(yb)

    wtmp[...] = jnp.zeros_like(wtmp)
    ws[...] = jnp.zeros_like(ws)
    for ky in range(7):
        for c in range(chans):
            wtmp[pl.ds(8, 7), :] = w7_ref[ky, c].astype(F32)
            taps = [wtmp[pl.ds(7 - 2 * q, 16), :] for q in range(4)]
            ws[pl.ds((ky + 1) * 64 + c * 16, 16), :] = jnp.concatenate(taps, axis=1).astype(BF16)

    @pl.loop(0, layers)
    def _(l):
        for r in range(4):
            for slot, t in enumerate((1, 2, 3, 0)):
                for dy in range(2):
                    ky = r - dy
                    parts = []
                    for dx in range(2):
                        kx = t - dx
                        if 0 <= ky < 3 and 0 <= kx < 3:
                            parts.append(wa_ref[l, ky, kx])
                        else:
                            parts.append(jnp.zeros((64, 64), BF16))
                    wat[l, pl.ds(r * 256 + slot * 64, 64), pl.ds(dy * 128, 128)] = jnp.concatenate(parts, axis=1)

    for r in range(3):
        for slot, kx in enumerate((1, 2, None, 0)):
            wdt[pl.ds(r * 256 + slot * 64, 64), :] = jnp.zeros((64, 128), BF16) if kx is None else wd_ref[r, kx]

    def clear_acc():
        acc[...] = jnp.zeros_like(acc)

    def add_acc(parts):
        s, q = acc[0], acc[1]
        for z in parts:
            z3 = z.reshape(z.shape[0] // 8, 8, z.shape[1])
            s = s + jnp.sum(z3, axis=0)
            q = q + jnp.sum(z3 * z3, axis=0)
        acc[0] = s
        acc[1] = q

    def stat_copy(par, k, source):
        block = slots.at[par, source]
        return pltpu.make_async_remote_copy(
            src_ref=block, dst_ref=block, send_sem=ssend.at[par, k], recv_sem=srecv.at[par, k],
            device_id={"sp": lax.rem(me + k, group)})

    def reduce_stats(par, bn, count, fold, then=None):
        s = jnp.sum(acc[0], axis=0, keepdims=True)
        q = jnp.sum(acc[1], axis=0, keepdims=True)
        slots[par, me] = jnp.concatenate([s, q, jnp.zeros((6, 128), F32)], axis=0)
        for k in range(1, group):
            stat_copy(par, k, me).start()
        if then is not None:
            then()
        for k in range(1, group):
            stat_copy(par, k, lax.rem(me + group - k, group)).wait_recv()
        for k in range(1, group):
            stat_copy(par, k, me).wait_send()
        total = slots[par, 0]
        for d in range(1, group):
            total = total + slots[par, d]
        if fold:
            total = total + half_swap(total)
            bn = jnp.concatenate([bn, bn], axis=1)
        mean = total[0:1] / count
        var = total[1:2] / count - mean * mean
        scale = bn[0:1] * lax.rsqrt(var + BN_EPS)
        return mean, scale, bn[1:2]

    def apply(z, coef):
        mean, scale, beta = coef
        return jnp.maximum((z - mean) * scale + beta, 0.0)

    early = zr.shape[1]
    pieces = ((1, early), (1 + early, cols // 2 + 2 - early), (cols // 2 + 3, cols // 2 - 2), (1, cols))

    def halo(buf, n, side, which):
        src, dst, dev = (1, n + 1, up) if side == 0 else (n, 0, down)
        where = pl.ds(*pieces[which])
        return pltpu.make_async_remote_copy(
            src_ref=buf.at[src, where], dst_ref=buf.at[dst, where], send_sem=hsend.at[which], recv_sem=hrecv.at[which],
            device_id={"sp": dev})

    far_up, far_down = jnp.logical_and(even, has_up), jnp.logical_and(odd, has_down)
    near_up, near_down = jnp.logical_and(odd, has_up), jnp.logical_and(even, has_down)

    def far_op(op):
        @pl.when(far_up)
        def _():
            op(0, 1)

        @pl.when(far_down)
        def _():
            op(1, 0)

    def near_op(op):
        @pl.when(near_up)
        def _():
            op(0, 1)

        @pl.when(near_down)
        def _():
            op(1, 0)

    def start_far(buf, n, which):
        far_op(lambda out, back: [halo(buf, n, out, k).start() for k in which] and None)

    def wait_far(buf, n, which):
        far_op(lambda out, back: halo(buf, n, back, which).wait_recv())

    def sent_far(buf, n, which):
        far_op(lambda out, back: [halo(buf, n, out, k).wait_send() for k in which] and None)

    def start_near(buf, n):
        near_op(lambda out, back: halo(buf, n, out, 3).start())

    def wait_near(buf, n):
        near_op(lambda out, back: halo(buf, n, back, 3).wait_recv())

    def drain_halos(buf, n):
        sent_far(buf, n, (1, 2))
        near_op(lambda out, back: halo(buf, n, out, 3).wait_send())

    def early_copy(n, par, side):
        return pltpu.make_async_remote_copy(
            src_ref=za.at[0 if side == 0 else n - 1, pl.ds(0, early)], dst_ref=zr.at[par],
            send_sem=zsend.at[par], recv_sem=zrecv.at[par], device_id={"sp": up if side == 0 else down})

    def start_early(n, par):
        far_op(lambda out, back: early_copy(n, par, out).start())

    def finish_early(dst, n, par, coef):
        def take(out, back):
            early_copy(n, par, out).wait_recv()
            early_copy(n, par, out).wait_send()
            row = 0 if back == 1 else n + 1

            @pl.loop(0, early // 8)
            def _(jb):
                dst[row, pl.ds(jb * 8 + 1, 8)] = apply(zr[par, pl.ds(jb * 8, 8)], coef).astype(BF16)

        far_op(take)

    def far_near(n):
        return jnp.where(even, 0, n - 1), jnp.where(even, n - 1, 0)

    clear_acc()
    lanes = lax.broadcasted_iota(jnp.int32, (xpairs, nimg, 128), 2)

    def wait_pixels(m):
        @pl.when(has_up)
        def _():
            pix_down(m).wait_recv()

        @pl.when(has_down)
        def _():
            pix_up(m).wait_recv()

    wait_pixels(0)

    @pl.loop(0, 2 * chunks)
    def _(kk):
        first = lax.div(kk + 1, 2) - 1
        shift0 = 4 + 64 * lax.rem(kk, 2)

        @pl.when(jnp.logical_and(lax.rem(kk, 2) == 1, kk < 2 * chunks - 1))
        def _():
            wait_pixels(first + 1)

        low_ok = kk > 0
        high_ok = kk < 2 * chunks - 1
        left, right = jnp.maximum(first, 0), jnp.minimum(first + 1, chunks - 1)
        for r in range(2):
            for c in range(chans):
                off = r * 64 + c * 16
                rel = jnp.bitwise_and(lanes - off, 127)
                take_left = jnp.logical_and(rel < shift0, low_ok)
                take_right = jnp.logical_and(rel >= shift0, high_ok)
                shift = lax.rem(shift0 + off, 128)
                lv = pltpu.roll(xt[left, :, r, c], shift, 2)
                rv = pltpu.roll(xt[right, :, r, c], shift, 2)
                xw[r, c] = jnp.where(take_left, lv, jnp.where(take_right, rv, jnp.zeros_like(rv)))

        for jj in range(8):
            packed = None
            rel = jnp.bitwise_and(lanes - 8 * jj, 127)
            for r in range(2):
                for c in range(chans):
                    piece = xw[r, c]
                    packed = piece if packed is None else jnp.where(rel < r * 64 + c * 16, packed, piece)
            if jj:
                packed = pltpu.roll(packed, 128 - 8 * jj, 2)
            lhs = jnp.concatenate([packed[p:p + srows].reshape(srows * nimg, 128) for p in range(4)], axis=1)
            z = jnp.dot(lhs, ws[...], preferred_element_type=F32)
            j = kk * 8 + jj
            zl, zh = z[:, :128], z[:, 128:]
            zs[:, 0, pl.ds(j + 1, 1)] = zl.reshape(srows, 1, nimg, 128)
            zs[:, 1, pl.ds(j + 1, 1)] = zh.reshape(srows, 1, nimg, 128)
            add_acc([zl[nimg:], zh[nimg:]])

    for h in range(srows):
        zs[h, 1, 0] = jnp.zeros((nimg, 128), F32)

    coef = reduce_stats(0, bns_ref[...], cnt_s, True)

    jp = 8

    def pool_row(h, jb):
        a = apply(zs[h, 0, pl.ds(jb * jp + 1, jp)], coef).astype(BF16)
        b = apply(zs[h, 1, pl.ds(jb * jp, jp + 1)], coef)
        b = jnp.concatenate([jnp.where(jb > 0, b[:1], jnp.zeros_like(b[:1])), b[1:]], axis=0).astype(BF16)
        rb = half_swap(b)
        lo = low_half(a.shape)
        m = jnp.maximum(a, jnp.where(lo, half_swap(a), rb[1:]))
        return jnp.maximum(m, jnp.where(lo, rb[:jp], b[1:]))

    @pl.loop(0, cols // jp)
    def _(jb):
        top = pool_row(0, jb)
        hb[0, pl.ds(jb * jp, jp)] = jnp.where(has_up, top, jnp.zeros_like(top))

    def pool_pair(p):
        @pl.loop(0, cols // jp)
        def _(jb):
            top = pool_row(2 * p + 1, jb)
            bot = pool_row(2 * p + 2, jb)
            hb[p + 1, pl.ds(jb * jp, jp)] = bot
            ya[p + 1, pl.ds(jb * jp + 1, jp)] = jnp.maximum(top, bot)

    def pool_join(p):
        @pl.loop(0, cols // jp)
        def _(jb):
            old = ya[p + 1, pl.ds(jb * jp + 1, jp)]
            ya[p + 1, pl.ds(jb * jp + 1, jp)] = jnp.maximum(old, hb[p, pl.ds(jb * jp, jp)])

    far, near = far_near(rows)

    @pl.loop(0, 2)
    def _(t):
        pool_pair(jnp.where(even, t, rows - 2 + t))

    pool_join(far)
    start_far(ya, rows, (0, 1, 2))

    @pl.loop(2, rows)
    def _(t):
        pool_pair(jnp.where(even, t, t - 2))

    pool_join(near)
    start_near(ya, rows)

    @pl.loop(1, rows - 1)
    def _(p):
        pool_join(p)

    @pl.when(has_down)
    def _():
        for m in range(chunks):
            pix_down(m).wait_send()

    @pl.when(has_up)
    def _():
        for m in range(chunks):
            pix_up(m).wait_send()

    wait_far(ya, rows, 0)
    sent_far(ya, rows, (0,))

    ja = cols // 2

    def conv_a(l, i, jb):
        parts = []
        lo = low_half((ja, nimg, 128))
        for r in range(4):
            row = 2 * i + r
            mid = ya[row, pl.ds(jb * ja + 1, ja)]
            left = ya[row, pl.ds(jb * ja, ja)]
            right = ya[row, pl.ds(jb * ja + 2, ja)]
            parts.append(mid.reshape(ja * nimg, 128))
            parts.append(jnp.where(lo, right, left).reshape(ja * nimg, 128))
        z = jnp.dot(jnp.concatenate(parts, axis=1), wat[l], preferred_element_type=F32)
        for dy in range(2):
            za[2 * i + dy, pl.ds(jb * ja, ja)] = z[:, dy * 128:(dy + 1) * 128].reshape(ja, nimg, 128)
        add_acc([z[:, :128], z[:, 128:]])

    def norm_row(dst, row, coef):
        @pl.loop(0, cols // jp)
        def _(jb):
            dst[row + 1, pl.ds(jb * jp + 1, jp)] = apply(za[row, pl.ds(jb * jp, jp)], coef).astype(BF16)

    def norm_and_send(dst, n, coef, par):
        far, near = far_near(n)
        norm_row(dst, far, coef)
        start_far(dst, n, (1, 2))
        norm_row(dst, near, coef)
        start_near(dst, n)

        @pl.loop(1, n - 1)
        def _(row):
            norm_row(dst, row, coef)

        finish_early(dst, n, par, coef)

    def banded(conv, buf, n, blocks):
        far, near = far_near(blocks)

        @pl.loop(0, 2 * (blocks - 2))
        def _(s):
            conv(1 + lax.div(s, 2), lax.rem(s, 2))

        wait_near(buf, n)

        @pl.loop(0, 2)
        def _(s):
            conv(near, s)

        @pl.loop(0, 2)
        def _(s):
            @pl.when(s == 0)
            def _():
                wait_far(buf, n, 1)

            @pl.when(s == 1)
            def _():
                wait_far(buf, n, 2)

            conv(far, s)

        drain_halos(buf, n)

    @pl.loop(0, layers)
    def _(l):
        clear_acc()
        banded(functools.partial(conv_a, l), ya, rows, rows // 2)
        par = lax.rem(l + 1, 2)
        coef = reduce_stats(par, bna_ref[l], cnt_a, True, lambda: start_early(rows, par))
        norm_and_send(ya, rows, coef, par)

    clear_acc()
    jd = cols // 2

    def conv_d(i, jb):
        parts = []
        for r in range(3):
            row = 2 * i + r
            parts.append(ya[row, pl.ds(jb * jd + 1, jd)].reshape(jd * nimg, 128))
            parts.append(ya[row, pl.ds(jb * jd, jd)].reshape(jd * nimg, 128))
        z = jnp.dot(jnp.concatenate(parts, axis=1), wdt[...], preferred_element_type=F32)
        za[i, pl.ds(jb * jd, jd)] = z.reshape(jd, nimg, 128)
        add_acc([z])

    banded(conv_d, ya, rows, orows)
    par = (layers + 1) % 2
    coef = reduce_stats(par, bnd_ref[...], cnt_b, False, lambda: start_early(orows, par))

    def conv_b(l, i, jb):
        parts = []
        for r in range(3):
            for t in range(3):
                parts.append(yb[i + r, pl.ds(jb * jd + t, jd)].reshape(jd * nimg, 128))
        z = jnp.dot(jnp.concatenate(parts, axis=1), wb_ref[l], preferred_element_type=F32)
        za[i, pl.ds(jb * jd, jd)] = z.reshape(jd, nimg, 128)
        add_acc([z])

    for l in range(wb_ref.shape[0]):
        norm_and_send(yb, orows, coef, par)
        clear_acc()
        banded(functools.partial(conv_b, l), yb, orows, orows)
        par = 1 - par
        last = l == wb_ref.shape[0] - 1
        coef = reduce_stats(par, bnb_ref[l], cnt_b, False, None if last else lambda: start_early(orows, par))

    @pl.loop(0, orows)
    def _(row):
        for jb in range(cols // jp):
            y = apply(za[row, pl.ds(jb * jp, jp)], coef)
            out_ref[:, row, pl.ds(jb * jp, jp)] = jnp.transpose(y, (1, 0, 2)).astype(BF16)


def solution(mesh):
    group = mesh.shape["sp"]

    def local_stack(pixels, w_stem, bn_stem, w_a, bn_a, w_down, bn_down, w_b, bn_b):
        n, h, w, chans = pixels.shape
        rows, cols, orows = h // 4, w // 8, h // 8
        counts = (float(n * (h // 2) * group * (w // 2)), float(n * rows * group * (w // 4)), float(n * orows * group * (w // 8)))
        vm = pl.BlockSpec(memory_space=pltpu.VMEM)
        return pl.pallas_call(
            functools.partial(whole_kernel, group, counts),
            out_shape=jax.ShapeDtypeStruct((n, orows, cols, 128), BF16),
            in_specs=[vm] * 9,
            out_specs=vm,
            scratch_shapes=[
                pltpu.VMEM((w // 128, h // 2 + 4, 2, chans, n, 128), BF16),
                pltpu.VMEM((2, chans, h // 2 + 4, n, 128), BF16),
                pltpu.VMEM((h // 2 + 1, 2, cols + 1, n, 128), F32),
                pltpu.VMEM((rows, cols, n, 128), F32),
                pltpu.VMEM((2, cols // 2 - 8, n, 128), F32),
                pltpu.VMEM((rows + 2, cols + 2, n, 128), BF16),
                pltpu.VMEM((rows + 1, cols, n, 128), BF16),
                pltpu.VMEM((orows + 2, cols + 2, n, 128), BF16),
                pltpu.VMEM((32, 64), F32),
                pltpu.VMEM((512, 256), BF16),
                pltpu.VMEM((w_a.shape[0], 1024, 256), BF16),
                pltpu.VMEM((768, 128), BF16),
                pltpu.VMEM((2, 8, 128), F32),
                pltpu.VMEM((2, group, 8, 128), F32),
                pltpu.SemaphoreType.DMA((2, group)),
                pltpu.SemaphoreType.DMA((2, group)),
                pltpu.SemaphoreType.DMA((4,)),
                pltpu.SemaphoreType.DMA((4,)),
                pltpu.SemaphoreType.DMA((2, w // 128)),
                pltpu.SemaphoreType.DMA((2, w // 128)),
                pltpu.SemaphoreType.DMA((2,)),
                pltpu.SemaphoreType.DMA((2,)),
            ],
            compiler_params=pltpu.CompilerParams(collective_id=0, has_side_effects=True, vmem_limit_bytes=67_000_000),
        )(pixels.transpose(0, 3, 1, 2), w_stem.transpose(0, 2, 1, 3), w_a, w_down, w_b.reshape(w_b.shape[0], 9 * 128, 128),
          bn_stem, bn_a, bn_down, bn_b)

    return jax.shard_map(local_stack, mesh=mesh, in_specs=(P("dp", "sp"),) + (P(),) * 8, out_specs=P("dp", "sp"), check_vma=False)
```

time: 264 us -> 160 us (0.61)
  Pallas kernels: 201 us -> 157 us
  local copies, waits for them, and re-layouts: 38.7 us -> 2.67 us
  other arithmetic: 14.8 us -> 0 us
  starting transfers between devices: 7.92 us -> 0 us
    pallas_call x1, Pallas kernels: 201 us -> 157 us  [local_stack(): pl.pallas_call(functools.partial(whole_kernel, group, counts), out_shape=...]
    reshape x2 -> x0, local copies, waits for them, and re-layouts: 19.9 us -> none  [local_stack(): x.reshape(chans, hp, 2, n, (w + 64) // 64, 64).transpose(4, 0, 2, 1, 3, 5)]
    concatenate x3 -> x0, other arithmetic: 14.8 us -> none  [the longest x1 10.1 us: local_stack(): xk = jnp.concatenate([x[:-1], x[1:]], axis=-1)]
    slice x3 -> x0, local copies, waits for them, and re-layouts: 8.03 us -> none  [the longest x1 5.45 us: local_stack(): xk = jnp.concatenate([x[:-1], x[1:]], axis=-1)]
    ppermute x2 -> x0, starting transfers between devices: 7.92 us -> none  [the longest x1 5.1 us: local_stack(): lax.ppermute(x[:, -3:], 'sp', [(i, i + 1) for i in range(group - 1)])]
    pad x2 -> x0, local copies, waits for them, and re-layouts: 4.89 us -> none  [the longest x1 4.09 us: local_stack(): x = jnp.pad(x, ((0, 0), (0, 0), (0, 0), (4, 60)))]
    transpose x1 -> x0, local copies, waits for them, and re-layouts: 3.16 us -> none  [local_stack(): return out.transpose(2, 0, 1, 3)]
    another operation x4 -> x0, local copies, waits for them, and re-layouts: 2.73 us -> none  [the longest x2 1.38 us: local_stack(): jnp.tile(bn_a, (1, 1, 2))]
  transfers between devices with their start and end apart: 2 -> 0, of which waited for: 0 -> 0; matrix products, arithmetic and copies ran while one was open for 2% -> 0% of each run, Pallas kernels for 0% -> 0%
where the time goes in v2:
time: 160 us
  Pallas kernels  157 us (98%)
  local copies, waits for them, and re-layouts  2.67 us (2%)
    pallas_call x1, Pallas kernels, local_stack(): pl.pallas_call(functools.partial(whole_kernel, group, counts), out_shape=...  157 us

profile of v2, /device:TPU:21, one launch (start us, length us, event | category | flops | bytes accessed | tf_op | source)
XLA Modules:
  0.0 160.0 jit_solution(7598206798440886216)
XLA Ops:
  0.0 157.3 %shard_map.91 = bf16[32,3,64,128]{3,2,1,0:T(8,128)(2,1)} custom-call(bf16[32,3,24,512]{3,2,1,0:T(8,128)(2,1)} %bitcast.3, bf16[7,3,7,64]{3,2,1,0:T(8,128)(2,1)} %bitcast.5, bf16[6,3,3,64,64]{4,3,2,1,0:T(8,128)(2,1)} %wa_ref.1, bf16[3,3,64,128]{3,2,1,0:T(8,128)(2,1)} %wd_ref.1, bf16[2,1152,128]{2,1,0:T(8,128)(2,1)} %bitcast.4, f32[2,64]{1,0:T(2,128)} %bns_ref.1, ...), custom_call_target="tpu_custom_call" | custom-call | tf_op jit(solution)/shard_map/pallas_call | solution.py:475
  157.3 2.7 %copy.11 = bf16[32,3,64,128]{3,2,1,0:T(8,128)(2,1)} copy(bf16[32,3,64,128]{3,2,1,0:T(8,128)(2,1)} %shard_map.91) | data formatting | bytes 3145728

commit v3 on v2

--- a/solution.py
+++ b/solution.py
@@ -134,8 +134,8 @@
     def reduce_stats(par, bn, count, fold, then=None):
         s = jnp.sum(acc[0], axis=0, keepdims=True)
         q = jnp.sum(acc[1], axis=0, keepdims=True)
-        slots[par, me] = jnp.concatenate([s, q, jnp.zeros((6, 128), F32)], axis=0)
-        for k in range(1, group):
+        slots[par, me] = jnp.concatenate([s, q], axis=0)
+        for k in sorted(range(1, group), key=lambda d: abs(2 * d - group)):
             stat_copy(par, k, me).start()
         if then is not None:
             then()
@@ -375,7 +375,7 @@
         def _(jb):
             dst[row + 1, pl.ds(jb * jp + 1, jp)] = apply(za[row, pl.ds(jb * jp, jp)], coef).astype(BF16)
 
-    def norm_and_send(dst, n, coef, par):
+    def norm_and_send(dst, n, coef):
         far, near = far_near(n)
         norm_row(dst, far, coef)
         start_far(dst, n, (1, 2))
@@ -386,9 +386,7 @@
         def _(row):
             norm_row(dst, row, coef)
 
-        finish_early(dst, n, par, coef)
-
-    def banded(conv, buf, n, blocks):
+    def banded(conv, buf, n, blocks, arrived=None):
         far, near = far_near(blocks)
 
         @pl.loop(0, 2 * (blocks - 2))
@@ -400,6 +398,9 @@
         @pl.loop(0, 2)
         def _(s):
             conv(near, s)
+
+        if arrived is not None:
+            arrived()
 
         @pl.loop(0, 2)
         def _(s):
@@ -415,15 +416,23 @@
 
         drain_halos(buf, n)
 
-    @pl.loop(0, layers)
-    def _(l):
-        clear_acc()
-        banded(functools.partial(conv_a, l), ya, rows, rows // 2)
+    def finish_a(l):
         par = lax.rem(l + 1, 2)
         coef = reduce_stats(par, bna_ref[l], cnt_a, True, lambda: start_early(rows, par))
-        norm_and_send(ya, rows, coef, par)
+        norm_and_send(ya, rows, coef)
+        clear_acc()
+        return lambda: finish_early(ya, rows, par, coef)
 
     clear_acc()
+    banded(functools.partial(conv_a, 0), ya, rows, rows // 2)
+
+    @pl.loop(1, layers)
+    def _(l):
+        arrived = finish_a(l - 1)
+        banded(functools.partial(conv_a, l), ya, rows, rows // 2, arrived)
+
+    arrived = finish_a(layers - 1)
+
     jd = cols // 2
 
     def conv_d(i, jb):
@@ -436,7 +445,7 @@
         za[i, pl.ds(jb * jd, jd)] = z.reshape(jd, nimg, 128)
         add_acc([z])
 
-    banded(conv_d, ya, rows, orows)
+    banded(conv_d, ya, rows, orows, arrived)
     par = (layers + 1) % 2
     coef = reduce_stats(par, bnd_ref[...], cnt_b, False, lambda: start_early(orows, par))
 
@@ -450,9 +459,9 @@
         add_acc([z])
 
     for l in range(wb_ref.shape[0]):
-        norm_and_send(yb, orows, coef, par)
+        norm_and_send(yb, orows, coef)
         clear_acc()
-        banded(functools.partial(conv_b, l), yb, orows, orows)
+        banded(functools.partial(conv_b, l), yb, orows, orows, functools.partial(finish_early, yb, orows, par, coef))
         par = 1 - par
         last = l == wb_ref.shape[0] - 1
         coef = reduce_stats(par, bnb_ref[l], cnt_b, False, None if last else lambda: start_early(orows, par))
@@ -491,7 +500,7 @@
                 pltpu.VMEM((w_a.shape[0], 1024, 256), BF16),
                 pltpu.VMEM((768, 128), BF16),
                 pltpu.VMEM((2, 8, 128), F32),
-                pltpu.VMEM((2, group, 8, 128), F32),
+                pltpu.VMEM((2, group, 2, 128), F32),
                 pltpu.SemaphoreType.DMA((2, group)),
                 pltpu.SemaphoreType.DMA((2, group)),
                 pltpu.SemaphoreType.DMA((4,)),

time: 160 us -> 152 us (0.950)
  Pallas kernels: 157 us -> 149 us
    pallas_call x1, Pallas kernels: 157 us -> 149 us  [local_stack(): pl.pallas_call(functools.partial(whole_kernel, group, counts), out_shape=...]
where the time goes in v3:
time: 152 us
  Pallas kernels  149 us (98%)
  local copies, waits for them, and re-layouts  2.67 us (2%)
    pallas_call x1, Pallas kernels, local_stack(): pl.pallas_call(functools.partial(whole_kernel, group, counts), out_shape=...  149 us

profile of v3, /device:TPU:21, one launch (start us, length us, event | category | flops | bytes accessed | tf_op | source)
XLA Modules:
  0.0 151.7 jit_solution(10575933870938766445)
XLA Ops:
  0.0 149.0 %shard_map.91 = bf16[32,3,64,128]{3,2,1,0:T(8,128)(2,1)} custom-call(bf16[32,3,24,512]{3,2,1,0:T(8,128)(2,1)} %bitcast.3, bf16[7,3,7,64]{3,2,1,0:T(8,128)(2,1)} %bitcast.5, bf16[6,3,3,64,64]{4,3,2,1,0:T(8,128)(2,1)} %wa_ref.1, bf16[3,3,64,128]{3,2,1,0:T(8,128)(2,1)} %wd_ref.1, bf16[2,1152,128]{2,1,0:T(8,128)(2,1)} %bitcast.4, f32[2,64]{1,0:T(2,128)} %bns_ref.1, ...), custom_call_target="tpu_custom_call" | custom-call | tf_op jit(solution)/shard_map/pallas_call | solution.py:484
  149.0 2.7 %copy.11 = bf16[32,3,64,128]{3,2,1,0:T(8,128)(2,1)} copy(bf16[32,3,64,128]{3,2,1,0:T(8,128)(2,1)} %shard_map.91) | data formatting | bytes 3145728
